TPU v7x, 256 devices: a 8x8x2 block of a 8x8x16 slice. The times are simulated.
256 devices in a mesh: grp: 2 (over z), chan: 128 (over y, x, core).
Axes of the slice: x: 8, y: 8, z: 2, core: 2. Of those that a mesh axis runs over, the one named last changes fastest.
The devices are a block of a 8x8x16 slice.
Arguments:
- voltages: bfloat16 [8192, 2, 64, 128], P(('grp', 'chan')), parts along dimension 0, may hold values from -9 to 9
- delays: float32 [512, 64], replicated, may hold values from -2 to 2
- pointing: int32 [256], P('grp'), parts along dimension 0, may hold values from 0 to 511
- dm_index: int32 [256], P(('grp', 'chan')), parts along dimension 0, may hold values from 0 to 511
- dish_mask: int32 [128], P('grp'), parts along dimension 0, may hold values 0 or 1
Outputs:
- dedispersed: float32 [256, 2, 128, 4096], P(('grp', 'chan')), parts along dimension 0
There are 2 independent parts, one for each index of `grp`. A program takes and returns all parts, laid end to end along the dimension named above; an argument that names none is the same for every part. Nothing has to cross between parts.
All inputs are finite; a program needn't handle non-finite values.
Results may differ from a plain program's by a relative error of at most 0.005.
Values may be sent and summed in bfloat16 or wider, within the bound.
A program may use at most 64 MiB of HBM per device.

v0:
```python
import functools
import math

import jax
import jax.numpy as jnp
import numpy as np
from jax import lax
from jax.experimental import pallas as pl
from jax.experimental.pallas import tpu as pltpu
from jax.sharding import PartitionSpec as P

CHANS = 4096
LOG_LEN = 19
LENGTH = 2**LOG_LEN
BAND_LOW = 0.856
BAND_WIDTH = 0.856
EPSILON = 1e-06
TWO_PI = 2.0 * math.pi
HIGHEST = lax.Precision.HIGHEST
MESH_ID = pl.DeviceIdType.MESH
VMEM_SPEC = pl.BlockSpec(memory_space=pltpu.VMEM)
SMEM_SPEC = pl.BlockSpec(memory_space=pltpu.SMEM)
ANY_SPEC = pl.BlockSpec(memory_space=pl.ANY)
LINES = 16
RADIX = 128


def circle(angle):
    square = angle * angle
    sine = angle * (
        1.0 + square * (-1.0 / 6 + square * (1.0 / 120 + square * (-1.0 / 5040 + square / 362880)))
    )
    cosine = 1.0 + square * (
        -0.5 + square * (1.0 / 24 + square * (-1.0 / 720 + square * (1.0 / 40320)))
    )
    return cosine, sine


def turned(cosine, sine, quarter):
    swap = (quarter & 1) != 0
    cos_out = jnp.where(swap, sine, cosine)
    sin_out = jnp.where(swap, cosine, sine)
    cos_out = jnp.where(((quarter + 1) & 2) != 0, -cos_out, cos_out)
    sin_out = jnp.where((quarter & 2) != 0, -sin_out, sin_out)
    return cos_out, sin_out


def circle_units(units):
    moved = units + LENGTH // 8
    quarter = (moved >> (LOG_LEN - 2)) & 3
    rest = (moved & (LENGTH // 4 - 1)) - LENGTH // 8
    cosine, sine = circle(rest.astype(jnp.float32) * (TWO_PI / LENGTH))
    return turned(cosine, sine, quarter)


def circle_turns(turns):
    quarters = jnp.floor(4.0 * turns + 0.5)
    cosine, sine = circle((turns - 0.25 * quarters) * TWO_PI)
    return turned(cosine, sine, quarters.astype(jnp.int32))


def times(a_re, a_im, b_re, b_im):
    return a_re * b_re - a_im * b_im, a_re * b_im + a_im * b_re


def four(values, sign):
    (a_re, a_im), (b_re, b_im), (c_re, c_im), (d_re, d_im) = values
    p_re, p_im = a_re + c_re, a_im + c_im
    q_re, q_im = a_re - c_re, a_im - c_im
    r_re, r_im = b_re + d_re, b_im + d_im
    t_re, t_im = b_re - d_re, b_im - d_im
    if sign > 0:
        t_re, t_im = -t_im, t_re
    else:
        t_re, t_im = t_im, -t_re
    return [
        (p_re + r_re, p_im + r_im),
        (q_re + t_re, q_im + t_im),
        (p_re - r_re, p_im - r_im),
        (q_re - t_re, q_im - t_im),
    ]


def sixteen(values, sign):
    result = [None] * 16
    inner = [four([values[4 * high + low] for high in range(4)], sign) for low in range(4)]
    for first in range(4):
        column = []
        for low in range(4):
            re_part, im_part = inner[low][first]
            power = low * first
            if power == 4:
                pair = (-im_part, re_part) if sign > 0 else (im_part, -re_part)
            elif power:
                angle = sign * TWO_PI * power / 16
                pair = times(re_part, im_part, math.cos(angle), math.sin(angle))
            else:
                pair = (re_part, im_part)
            column.append(pair)
        for second, pair in enumerate(four(column, sign)):
            result[first + 4 * second] = pair
    return result


def form_kernel(freq_ref, volt_ref, table_ref, row_ref, mask_ref, out_ref, wave, step):
    chans, rows, _ = out_ref.shape
    points = table_ref.shape[0]
    select = (
        lax.broadcasted_iota(jnp.int32, (points, rows), 0) == row_ref[...]
    ).astype(jnp.float32)
    delay = lax.dot_general(
        select, table_ref[...], (((0,), (0,)), ((), ())), precision=HIGHEST,
        preferred_element_type=jnp.float32,
    )
    delay = jnp.concatenate([delay, delay], 1)
    dishes = delay.shape[1] // 2
    part_out = lax.broadcasted_iota(jnp.int32, delay.shape, 0) & 1
    part_in = (lax.broadcasted_iota(jnp.int32, delay.shape, 1) >= dishes).astype(jnp.int32)
    offset = 0.25 * (part_in - part_out).astype(jnp.float32)
    gain = mask_ref[...].astype(jnp.float32) * (1.0 / math.sqrt(dishes))
    cosine, sine = circle_turns(freq_ref[0] * delay - offset)
    wave[0] = cosine * gain
    wave[1] = sine * gain
    cosine, sine = circle_turns((BAND_WIDTH / CHANS) * delay)
    step[0] = cosine
    step[1] = sine

    def one(chan, _):
        re_part = wave[0]
        im_part = wave[1]
        out_ref[chan] = jnp.dot(
            re_part.astype(jnp.bfloat16), volt_ref[chan], preferred_element_type=jnp.float32
        ).astype(jnp.bfloat16)
        re_next, im_next = times(re_part, im_part, step[0], step[1])
        wave[0] = re_next
        wave[1] = im_next
        return 0

    lax.fori_loop(0, chans, one, 0)


def exchange_kernel(
    sizes, rate_ref, src_ref, dst_ref, tw_ref, tm_ref, q_ref, em_ref, f_ref,
    send_sem, recv_sem,
):
    rows_y, rows_x, cores = sizes
    members = rows_y * rows_x * cores
    group = lax.axis_index("grp")
    me = lax.axis_index("chan")
    my_y = me // (rows_x * cores)
    my_x = (me // cores) % rows_x
    my_core = me % cores
    barrier = pltpu.get_barrier_semaphore()

    def greet(hop, _):
        pl.semaphore_signal(
            barrier, inc=1, device_id=(group, lax.rem(me + hop, members)),
            device_id_type=MESH_ID,
        )
        return 0

    lax.fori_loop(1, members, greet, 0)
    pl.semaphore_wait(barrier, members - 1)

    def send(hop, _):
        hop_x = (hop // cores) % rows_x
        hop_y = (hop // (cores * rows_x) + hop_x) % rows_y
        to_y = (my_y + hop_y) % rows_y
        to_x = (my_x + hop_x) % rows_x
        to = (to_y * rows_x + to_x) * cores + (my_core + hop) % cores
        pltpu.make_async_remote_copy(
            src_ref=src_ref.at[:, pl.ds(pl.multiple_of(2 * to, 2), 2)],
            dst_ref=dst_ref.at[:, pl.ds(pl.multiple_of(2 * me, 2), 2)],
            send_sem=send_sem,
            recv_sem=recv_sem,
            device_id=(group, to),
            device_id_type=MESH_ID,
        ).start()
        return 0

    lax.fori_loop(1, members, send, 0)

    rate = rate_ref[0]
    inverse = rate_ref[1]
    tables(rate, inverse, tw_ref, tm_ref, q_ref, em_ref, f_ref)

    whole = pltpu.make_async_remote_copy(
        src_ref=src_ref.at[:, pl.ds(0, 2 * (members - 1))],
        dst_ref=dst_ref.at[:, pl.ds(0, 2 * (members - 1))],
        send_sem=send_sem,
        recv_sem=recv_sem,
        device_id=(group, me),
        device_id_type=MESH_ID,
    )
    whole.wait_recv()
    whole.wait_send()
    block = pl.ds(pl.multiple_of((me // 8) * 16, 16), 16)
    shape = (src_ref.shape[0], 16, src_ref.shape[2])
    mine = lax.broadcasted_iota(jnp.int32, shape, 1) // 2 == me % 8
    dst_ref[:, block, :] = jnp.where(
        mine, src_ref[:, block, :].astype(jnp.float32), dst_ref[:, block, :].astype(jnp.float32)
    ).astype(jnp.bfloat16)


def tables(rate, inverse, tw_ref, tm_ref, q_ref, em_ref, f_ref):
    piece = 32

    def position(shape, axis):
        return lax.broadcasted_iota(jnp.int32, shape, axis)

    shape = (piece, RADIX)
    per = 2 * RADIX // piece

    def chan_turn(i, _):
        line, start = i // per, pl.multiple_of((i % per) * piece, piece)
        row = position(shape, 0) + start
        low = row & (RADIX - 1)
        chan_unit = line * (2 * low + row // RADIX) * (LENGTH // CHANS)
        cosine, sine = circle_units(
            chan_unit + inverse * (position(shape, 1) * low) * (LENGTH // RADIX)
        )
        tw_ref[0, line, pl.ds(start, piece)] = cosine
        tw_ref[1, line, pl.ds(start, piece)] = sine
        return 0

    lax.fori_loop(0, LINES * per, chan_turn, 0)

    wide = (piece, 2 * RADIX)
    per_wide = RADIX // piece

    def time_matrix(i, _):
        start = pl.multiple_of(i * piece, piece)
        time = position(wide, 0) + start
        beat = position(wide, 1) // 2
        parity = position(wide, 1) & 1
        cosine, sine = circle_units(-inverse * (time * beat) * (LENGTH // RADIX))
        for own in range(2):
            keep = parity == own
            re_part = jnp.where(keep, cosine, 0.0)
            im_part = jnp.where(keep, sine, 0.0)
            from_re = pl.ds(start + 2 * own * RADIX, piece)
            from_im = pl.ds(start + (2 * own + 1) * RADIX, piece)
            tm_ref[from_re, : 2 * RADIX] = re_part.astype(jnp.bfloat16)
            tm_ref[from_re, 2 * RADIX :] = im_part.astype(jnp.bfloat16)
            tm_ref[from_im, : 2 * RADIX] = (-im_part).astype(jnp.bfloat16)
            tm_ref[from_im, 2 * RADIX :] = re_part.astype(jnp.bfloat16)
        return 0

    lax.fori_loop(0, per_wide, time_matrix, 0)

    def wide_turn(i, _):
        line, start = i // per_wide, pl.multiple_of((i % per_wide) * piece, piece)
        low = position(wide, 0) + start
        beat = position(wide, 1) // 2
        here = pl.ds(start, piece)
        cosine, sine = circle_units(
            inverse
            * (
                low * (low - 2 * beat)
                + line * line * (LENGTH // 32)
                + line * (low - beat) * (LENGTH // 2048)
            )
        )
        q_ref[0, line, here] = cosine
        q_ref[1, line, here] = sine
        cosine, sine = circle_units(
            inverse
            * (
                beat * (beat + line * (LENGTH // 2048) + low * (LENGTH // RADIX))
                + line * line * (LENGTH // 32)
            )
            - rate * (LENGTH // 8)
        )
        f_ref[0, line, here] = cosine
        f_ref[1, line, here] = sine
        return 0

    lax.fori_loop(0, LINES * per_wide, wide_turn, 0)

    def end_matrix(i, _):
        line, start = i // per_wide, pl.multiple_of((i % per_wide) * piece, piece)
        high = position(shape, 0) + start
        cosine, sine = circle_units(
            -inverse * (position(shape, 1) * (LINES * high + line)) * (LENGTH // 2048)
        )
        upper = pl.ds(start, piece)
        lower = pl.ds(start + RADIX, piece)
        em_ref[line, upper, :RADIX] = cosine.astype(jnp.bfloat16)
        em_ref[line, upper, RADIX:] = (-sine).astype(jnp.bfloat16)
        em_ref[line, lower, :RADIX] = sine.astype(jnp.bfloat16)
        em_ref[line, lower, RADIX:] = cosine.astype(jnp.bfloat16)
        return 0

    lax.fori_loop(0, LINES * per_wide, end_matrix, 0)


def chain_kernel(
    rate_ref, x_ref, am_ref, tw_ref, tm_ref, q_ref, em_ref, f_ref, out_ref,
    grid, mid, held, total, sems,
):
    total[...] = jnp.zeros_like(total)
    for pair in range(LINES // 2):
        tops = [
            jnp.concatenate([x_ref[h * LINES + 2 * pair], x_ref[h * LINES + 2 * pair + 1]], 1)
            for h in range(2)
        ]
        data = jnp.concatenate(tops, 0)
        wide = data.astype(jnp.float32)
        total[...] += jnp.sum((wide * wide).reshape(-1, 8, 2 * RADIX), 0)
        mixed = jnp.dot(am_ref[...], data, preferred_element_type=jnp.float32)
        grid[2 * pair] = mixed[:, :RADIX]
        grid[2 * pair + 1] = mixed[:, RADIX:]

    def chan_lines(i, _):
        here = pl.ds(pl.multiple_of(i * 8, 8), 8)
        there = pl.ds(pl.multiple_of(i * 8 + 2 * RADIX, 8), 8)
        values = [
            times(grid[n, here], grid[n, there], tw_ref[0, n, here], tw_ref[1, n, here])
            for n in range(LINES)
        ]
        for n, (re_part, im_part) in enumerate(sixteen(values, 1)):
            grid[n, here] = re_part
            grid[n, there] = im_part
        return 0

    lax.fori_loop(0, 2 * RADIX // 8, chan_lines, 0)

    for quad in range(LINES // 4):
        rows = []
        for n in range(4 * quad, 4 * quad + 4):
            parts = [
                grid[n, part * 2 * RADIX + own * RADIX : part * 2 * RADIX + (own + 1) * RADIX]
                for own in range(2)
                for part in range(2)
            ]
            rows.append(jnp.concatenate(parts, 1).astype(jnp.bfloat16))
        mixed = jnp.dot(
            jnp.concatenate(rows, 0), tm_ref[...], preferred_element_type=jnp.float32
        )
        for n in range(4):
            mid[4 * quad + n] = mixed[n * RADIX : (n + 1) * RADIX]

    def beat_lines(i, _):
        here = pl.ds(pl.multiple_of(i * 8, 8), 8)
        for lane in range(0, 2 * RADIX, RADIX):
            re_at = slice(lane, lane + RADIX)
            im_at = slice(lane + 2 * RADIX, lane + 3 * RADIX)
            values = [
                times(
                    mid[n, here, re_at], mid[n, here, im_at],
                    q_ref[0, n, here, re_at], q_ref[1, n, here, re_at],
                )
                for n in range(LINES)
            ]
            for n, (re_part, im_part) in enumerate(sixteen(values, -1)):
                mid[n, here, re_at] = re_part
                mid[n, here, im_at] = im_part
        return 0

    lax.fori_loop(0, RADIX // 8, beat_lines, 0)

    power = jnp.sum(jnp.sum(total[...], 1, keepdims=True), 0, keepdims=True) * (1.0 / LENGTH)
    factor = lax.rsqrt(power + EPSILON) * (
        math.sqrt(2.0 / LENGTH) / math.sqrt(CHANS)
    )
    factor = jnp.broadcast_to(factor, (8, 2 * RADIX))[:1]
    copies = []
    for line in range(LINES):
        source = (rate_ref[1] * line) & (LINES - 1)
        data = jnp.concatenate(
            [mid[source, :, : 2 * RADIX], mid[source, :, 2 * RADIX :]], 0
        ).astype(jnp.bfloat16)
        mixed = jnp.dot(em_ref[line], data, preferred_element_type=jnp.float32)
        re_part, im_part = times(
            mixed[:RADIX], mixed[RADIX:], f_ref[0, line] * factor, f_ref[1, line] * factor
        )
        lanes = slice(line * 2 * RADIX, (line + 1) * 2 * RADIX)
        held[0, :, lanes] = re_part
        held[1, :, lanes] = im_part
        copy = pltpu.make_async_copy(
            held.at[:, :, pl.ds(line * 2 * RADIX, 2 * RADIX)],
            out_ref.at[0, :, :, pl.ds(line * 2 * RADIX, 2 * RADIX)],
            sems.at[line],
        )
        copy.start()
        copies.append(copy)
    for copy in copies:
        copy.wait()


def chan_matrix(members):
    n1 = np.arange(2 * RADIX)
    row_n1 = 2 * (n1 % RADIX) + n1 // RADIX
    half, member = np.meshgrid(np.arange(2), np.arange(members), indexing="ij")
    coarse = (2 * member + half).reshape(-1)
    angle = 2.0 * np.pi * ((row_n1[:, None] * coarse[None, :]) % (2 * RADIX)) / (2 * RADIX)
    cosine, sine = np.cos(angle), np.sin(angle)
    upper = np.stack([cosine, -sine], -1).reshape(2 * RADIX, -1)
    lower = np.stack([sine, cosine], -1).reshape(2 * RADIX, -1)
    return jnp.asarray(np.concatenate([upper, lower], 0), jnp.bfloat16)


def on_device(sizes, voltages, delays, pointing, dm_index, dish_mask):
    chan_dev, parts, dishes, samples = voltages.shape
    beams = pointing.shape[0]
    members = math.prod(sizes)
    rows = parts * beams
    first_chan = (lax.axis_index("chan") * chan_dev).astype(jnp.float32)
    frequency = (BAND_LOW + BAND_WIDTH * (first_chan + 0.5) / CHANS).reshape(1)
    rate = (2 * dm_index + 1).reshape(1)
    inverse = rate
    for _ in range(4):
        inverse = inverse * (2 - rate * inverse)
    rates = jnp.concatenate([rate, inverse & (LENGTH - 1)])
    block = jax.ShapeDtypeStruct((chan_dev, rows, samples), jnp.bfloat16)
    formed = pl.pallas_call(
        form_kernel,
        out_shape=block,
        in_specs=[SMEM_SPEC] + [VMEM_SPEC] * 4,
        out_specs=VMEM_SPEC,
        scratch_shapes=[pltpu.VMEM((2, rows, 2 * dishes), jnp.float32)] * 2,
        compiler_params=pltpu.CompilerParams(vmem_limit_bytes=12 << 20),
        name="form",
    )(
        frequency,
        voltages.reshape(chan_dev, parts * dishes, samples),
        delays,
        jnp.repeat(pointing, 2).reshape(1, rows),
        jnp.tile(dish_mask, 2).reshape(1, 2 * dishes),
    )
    wide = 2 * RADIX
    received, tw, tm, q, em, f = pl.pallas_call(
        functools.partial(exchange_kernel, sizes),
        out_shape=[
            block,
            jax.ShapeDtypeStruct((2, LINES, wide, samples), jnp.float32),
            jax.ShapeDtypeStruct((2 * wide, 2 * wide), jnp.bfloat16),
            jax.ShapeDtypeStruct((2, LINES, RADIX, wide), jnp.float32),
            jax.ShapeDtypeStruct((LINES, wide, wide), jnp.bfloat16),
            jax.ShapeDtypeStruct((2, LINES, RADIX, wide), jnp.float32),
        ],
        in_specs=[SMEM_SPEC, VMEM_SPEC],
        out_specs=[VMEM_SPEC] * 6,
        scratch_shapes=[pltpu.SemaphoreType.DMA(())] * 2,
        compiler_params=pltpu.CompilerParams(
            collective_id=0, has_side_effects=True, vmem_limit_bytes=24 << 20
        ),
        name="exchange",
    )(rates, formed)
    return pl.pallas_call(
        chain_kernel,
        out_shape=jax.ShapeDtypeStruct((1, 2, samples, CHANS), jnp.float32),
        in_specs=[SMEM_SPEC] + [VMEM_SPEC] * 7,
        out_specs=ANY_SPEC,
        scratch_shapes=[
            pltpu.VMEM((LINES, 2 * wide, samples), jnp.float32),
            pltpu.VMEM((LINES, RADIX, 2 * wide), jnp.float32),
            pltpu.VMEM((2, samples, CHANS), jnp.float32),
            pltpu.VMEM((8, wide), jnp.float32),
            pltpu.SemaphoreType.DMA((LINES,)),
        ],
        compiler_params=pltpu.CompilerParams(vmem_limit_bytes=36 << 20),
        name="chain",
    )(rates, received, chan_matrix(members), tw, tm, q, em, f)


def solution(mesh):
    members = mesh.shape["chan"]
    cores = 2
    side = math.isqrt(members // cores)
    sizes = (members // cores // side, side, cores)
    placed = (P(("grp", "chan")), P(), P("grp"), P(("grp", "chan")), P("grp"))
    return jax.shard_map(
        functools.partial(on_device, sizes),
        mesh=mesh,
        in_specs=placed,
        out_specs=P(("grp", "chan")),
        check_vma=False,
    )
```

profile of v0, /device:TPU:721, one launch (start us, length us, event | category | flops | bytes accessed | tf_op | source)
XLA Modules:
  0.0 101.7 jit_solution(6927683862447952961)
XLA Ops:
  0.0 0.0 copy-start.1
  0.7 0.1 pad_add_fusion.rate_ref
  0.8 0.7 tile.2
  1.5 0.1 reshape_tile.3.mask_ref
  1.5 0.7 broadcast_in_dim.3
  2.3 0.1 reshape_reshape.3.row_ref
  2.4 1.0 %copy.8.table_ref = f32[512,64]{1,0:T(8,128)S(1)} copy(f32[512,64]{0,1:T(8,128)} %param.7) | data formatting | bytes 262144 | tf_op args[1]
  3.5 0.0 copy-start
  3.5 1.2 %copy-done = bf16[32,2,64,128]{3,2,1,0:T(8,128)(2,1)S(1)} copy-done((bf16[32,2,64,128]{3,2,1,0:T(8,128)(2,1)S(1)}, bf16[32,2,64,128]{3,2,1,0:T(8,128)(2,1)}, u32[]{:S(2)}) %copy-start) | copy-done | bytes 1048600
  4.7 6.3 %form.1.src_ref = bf16[32,256,128]{2,1,0:T(8,128)(2,1)S(1)} custom-call(f32[1]{0:T(128)} %bitcast.freq_ref, bf16[32,128,128]{2,1,0:T(8,128)(2,1)S(1)} %bitcast.2, f32[512,64]{1,0:T(8,128)S(1)} %copy.8.table_ref, s32[1,256]{1,0:T(1,128)S(1)} %reshape_reshape.3.row_ref, s32[1,128]{1,0:T(1,128)S(1)} %reshape_tile.3.mask_ref), custom_call_target="tpu_custom_call" | custom-call | tf_op jit(solution)/shard_map/form/pallas_call | solution.py:416
  11.0 81.4 %exchange.1 = (bf16[32,256,128]{2,1,0:T(8,128)(2,1)S(1)}, f32[2,16,256,128]{3,2,1,0:T(8,128)S(1)}, bf16[512,512]{1,0:T(8,128)(2,1)S(1)}, f32[2,16,128,256]{3,2,1...) custom-call(s32[2]{0:T(128)S(1)} %pad_add_fusion.rate_ref, ...), custom_call_target="tpu_custom_call" | custom-call | tf_op jit(solution)/shard_map/exchange/pallas_call | solution.py:432
  92.3 0.0 copy-done.1
  92.3 9.4 %chain.1 = f32[1,2,128,4096]{3,2,1,0:T(8,128)} custom-call(s32[2]{0:T(128)S(1)} %pad_add_fusion.rate_ref, bf16[32,256,128]{2,1,0:T(8,128)(2,1)S(1)} %get-tuple-element.11.x_ref, bf16[512,512]{1,0:T(8,128)(2,1)S(1)} %copy-done.1, f32[2,16,256,128]{3,2,1,0:T(8,128)S(1)} %get-tuple-element.12.tw_ref, bf16[512,512]{1,0:T(8,128)(2,1)S(1)} %get-tuple-element.13.tm_ref, ...), custom_call_target="tpu_custom_call" | custom-call | tf_op jit(solution)/shard_map/chain/pallas_call | solution.py:450
Async XLA Ops:
  0.0 92.3 %copy-start.1 = (bf16[512,512]{1,0:T(8,128)(2,1)S(1)}, bf16[512,512]{1,0:T(8,128)(2,1)}, u32[]{:S(2)}) copy-start(bf16[512,512]{1,0:T(8,128)(2,1)} %constant.22.clone.am_ref) | copy-start | bytes 1572868
  3.5 1.2 %copy-start = (bf16[32,2,64,128]{3,2,1,0:T(8,128)(2,1)S(1)}, bf16[32,2,64,128]{3,2,1,0:T(8,128)(2,1)}, u32[]{:S(2)}) copy-start(bf16[32,2,64,128]{3,2,1,0:T(8,128)(2,1)} %param.6) | copy-start | bytes 3145732
where the time goes:
time: 102 us
  Pallas kernels  97 us (95%)
  local copies, waits for them, and re-layouts  3.87 us (4%)
    pallas_call x1, Pallas kernels, on_device(): pl.pallas_call(functools.partial(exchange_kernel, sizes), out_shape=[bloc...  81.4 us
    pallas_call x1, Pallas kernels, on_device(): pl.pallas_call(chain_kernel, out_shape=jax.ShapeDtypeStruct((1, 2, sample...  9.38 us
    pallas_call x1, Pallas kernels, on_device(): pl.pallas_call(form_kernel, out_shape=block, in_specs=[SMEM_SPEC] + [VMEM...  6.27 us
    unnamed x5, local copies, waits for them, and re-layouts  2.26 us

commit v1 on v0

--- a/solution.py
+++ b/solution.py
@@ -21,6 +21,7 @@
 VMEM_SPEC = pl.BlockSpec(memory_space=pltpu.VMEM)
 SMEM_SPEC = pl.BlockSpec(memory_space=pltpu.SMEM)
 ANY_SPEC = pl.BlockSpec(memory_space=pl.ANY)
+HBM_SPEC = pl.BlockSpec(memory_space=pltpu.HBM)
 LINES = 16
 RADIX = 128
 
@@ -102,104 +103,163 @@
     return result
 
 
-def form_kernel(freq_ref, volt_ref, table_ref, row_ref, mask_ref, out_ref, wave, step):
-    chans, rows, _ = out_ref.shape
-    points = table_ref.shape[0]
-    select = (
-        lax.broadcasted_iota(jnp.int32, (points, rows), 0) == row_ref[...]
-    ).astype(jnp.float32)
-    delay = lax.dot_general(
-        select, table_ref[...], (((0,), (0,)), ((), ())), precision=HIGHEST,
+def front_kernel(
+    sizes, rate_ref, freq_ref, point_ref, mask_ref, am_ref, volt_hbm, table_hbm,
+    grid_ref, total_ref, tw_ref, tm_ref, q_ref, em_ref, f_ref,
+    volt, table, wave, step, formed, landed, volt_sems, table_sem, send_sem, recv_sems,
+):
+    rows_y, rows_x, cores = sizes
+    members = rows_y * rows_x * cores
+    chunks = recv_sems.shape[0]
+    chunk = LINES // chunks
+    slots = 2 * chunk
+    group = lax.axis_index("grp")
+    me = lax.axis_index("chan")
+    my_y = me // (rows_x * cores)
+    my_x = (me // cores) % rows_x
+    my_core = me % cores
+
+    table_copy = pltpu.make_async_copy(table_hbm, table, table_sem)
+    table_copy.start()
+    volt_copies = []
+    for c in range(chunks):
+        pair = []
+        for half in range(2):
+            here = pl.ds(half * LINES + c * chunk, chunk)
+            copy = pltpu.make_async_copy(volt_hbm.at[here], volt.at[here], volt_sems.at[c, half])
+            copy.start()
+            pair.append(copy)
+        volt_copies.append(pair)
+
+    barrier = pltpu.get_barrier_semaphore()
+
+    def greet(hop, _):
+        pl.semaphore_signal(
+            barrier, inc=1, device_id=(group, lax.rem(me + hop, members)),
+            device_id_type=MESH_ID,
+        )
+        return 0
+
+    lax.fori_loop(1, members, greet, 0)
+
+    table_copy.wait()
+    rows = formed.shape[1]
+    points, beams = table.shape[1], rows // 2
+    select = lax.broadcasted_iota(jnp.int32, (points, beams), 0) == point_ref[...]
+    double = (
+        lax.broadcasted_iota(jnp.int32, (beams, rows), 1) // 2
+        == lax.broadcasted_iota(jnp.int32, (beams, rows), 0)
+    )
+    select = jnp.dot(
+        jnp.where(select, 1.0, 0.0).astype(jnp.bfloat16),
+        jnp.where(double, 1.0, 0.0).astype(jnp.bfloat16),
         preferred_element_type=jnp.float32,
     )
-    delay = jnp.concatenate([delay, delay], 1)
+    delay = jnp.dot(
+        table[...], select, precision=HIGHEST, preferred_element_type=jnp.float32
+    )
+    delay = jnp.concatenate([delay, delay], 0).T
     dishes = delay.shape[1] // 2
     part_out = lax.broadcasted_iota(jnp.int32, delay.shape, 0) & 1
     part_in = (lax.broadcasted_iota(jnp.int32, delay.shape, 1) >= dishes).astype(jnp.int32)
     offset = 0.25 * (part_in - part_out).astype(jnp.float32)
     gain = mask_ref[...].astype(jnp.float32) * (1.0 / math.sqrt(dishes))
-    cosine, sine = circle_turns(freq_ref[0] * delay - offset)
-    wave[0] = cosine * gain
-    wave[1] = sine * gain
+    gain = jnp.concatenate([gain, gain], 1)
+    for half in range(2):
+        start = freq_ref[0] + half * LINES * BAND_WIDTH / CHANS
+        cosine, sine = circle_turns(start * delay - offset)
+        wave[half, 0] = cosine * gain
+        wave[half, 1] = sine * gain
     cosine, sine = circle_turns((BAND_WIDTH / CHANS) * delay)
     step[0] = cosine
     step[1] = sine
 
-    def one(chan, _):
-        re_part = wave[0]
-        im_part = wave[1]
-        out_ref[chan] = jnp.dot(
-            re_part.astype(jnp.bfloat16), volt_ref[chan], preferred_element_type=jnp.float32
+    for c in range(chunks):
+        for copy in volt_copies[c]:
+            copy.wait()
+
+        def form(i, _, c=c):
+            for half in range(2):
+                re_part = wave[half, 0]
+                im_part = wave[half, 1]
+                formed[c * slots + half * chunk + i] = jnp.dot(
+                    re_part.astype(jnp.bfloat16),
+                    volt[half * LINES + c * chunk + i],
+                    preferred_element_type=jnp.float32,
+                ).astype(jnp.bfloat16)
+                re_next, im_next = times(re_part, im_part, step[0], step[1])
+                wave[half, 0] = re_next
+                wave[half, 1] = im_next
+            return 0
+
+        lax.fori_loop(0, chunk, form, 0)
+        if c == 0:
+            pl.semaphore_wait(barrier, members - 1)
+
+        def send(hop, _, c=c):
+            hop_x = (hop // cores) % rows_x
+            hop_y = (hop // (cores * rows_x) + hop_x) % rows_y
+            to_y = (my_y + hop_y) % rows_y
+            to_x = (my_x + hop_x) % rows_x
+            to = (to_y * rows_x + to_x) * cores + (my_core + hop) % cores
+            here = pl.ds(c * slots, slots)
+            pltpu.make_async_remote_copy(
+                src_ref=formed.at[here, pl.ds(pl.multiple_of(2 * to, 2), 2)],
+                dst_ref=landed.at[here, pl.ds(pl.multiple_of(2 * me, 2), 2)],
+                send_sem=send_sem,
+                recv_sem=recv_sems.at[c],
+                device_id=(group, to),
+                device_id_type=MESH_ID,
+            ).start()
+            return 0
+
+        lax.fori_loop(1, members, send, 0)
+
+    tables(rate_ref[0], rate_ref[1], tw_ref, tm_ref, q_ref, em_ref, f_ref)
+
+    total_ref[...] = jnp.zeros_like(total_ref)
+    block = pl.ds(pl.multiple_of((me // 8) * 16, 16), 16)
+    mine = lax.broadcasted_iota(jnp.int32, (slots, 16, formed.shape[2]), 1) // 2 == me % 8
+    most = pl.ds(0, 2 * (members - 1))
+    for c in range(chunks):
+        here = pl.ds(c * slots, slots)
+        pltpu.make_async_remote_copy(
+            src_ref=formed.at[here, most],
+            dst_ref=landed.at[here, most],
+            send_sem=send_sem,
+            recv_sem=recv_sems.at[c],
+            device_id=(group, me),
+            device_id_type=MESH_ID,
+        ).wait_recv()
+        landed[here, block, :] = jnp.where(
+            mine, formed[here, block, :].astype(jnp.float32),
+            landed[here, block, :].astype(jnp.float32),
         ).astype(jnp.bfloat16)
-        re_next, im_next = times(re_part, im_part, step[0], step[1])
-        wave[0] = re_next
-        wave[1] = im_next
-        return 0
-
-    lax.fori_loop(0, chans, one, 0)
-
-
-def exchange_kernel(
-    sizes, rate_ref, src_ref, dst_ref, tw_ref, tm_ref, q_ref, em_ref, f_ref,
-    send_sem, recv_sem,
-):
-    rows_y, rows_x, cores = sizes
-    members = rows_y * rows_x * cores
-    group = lax.axis_index("grp")
-    me = lax.axis_index("chan")
-    my_y = me // (rows_x * cores)
-    my_x = (me // cores) % rows_x
-    my_core = me % cores
-    barrier = pltpu.get_barrier_semaphore()
-
-    def greet(hop, _):
-        pl.semaphore_signal(
-            barrier, inc=1, device_id=(group, lax.rem(me + hop, members)),
-            device_id_type=MESH_ID,
-        )
-        return 0
-
-    lax.fori_loop(1, members, greet, 0)
-    pl.semaphore_wait(barrier, members - 1)
-
-    def send(hop, _):
-        hop_x = (hop // cores) % rows_x
-        hop_y = (hop // (cores * rows_x) + hop_x) % rows_y
-        to_y = (my_y + hop_y) % rows_y
-        to_x = (my_x + hop_x) % rows_x
-        to = (to_y * rows_x + to_x) * cores + (my_core + hop) % cores
-        pltpu.make_async_remote_copy(
-            src_ref=src_ref.at[:, pl.ds(pl.multiple_of(2 * to, 2), 2)],
-            dst_ref=dst_ref.at[:, pl.ds(pl.multiple_of(2 * me, 2), 2)],
-            send_sem=send_sem,
-            recv_sem=recv_sem,
-            device_id=(group, to),
-            device_id_type=MESH_ID,
-        ).start()
-        return 0
-
-    lax.fori_loop(1, members, send, 0)
-
-    rate = rate_ref[0]
-    inverse = rate_ref[1]
-    tables(rate, inverse, tw_ref, tm_ref, q_ref, em_ref, f_ref)
-
-    whole = pltpu.make_async_remote_copy(
-        src_ref=src_ref.at[:, pl.ds(0, 2 * (members - 1))],
-        dst_ref=dst_ref.at[:, pl.ds(0, 2 * (members - 1))],
+        for pair in range(chunk // 2):
+            first = c * slots + 2 * pair
+            data = jnp.concatenate(
+                [
+                    jnp.concatenate(
+                        [landed[first + half * chunk], landed[first + half * chunk + 1]], 1
+                    )
+                    for half in range(2)
+                ],
+                0,
+            )
+            wide = data.astype(jnp.float32)
+            total_ref[...] += jnp.sum((wide * wide).reshape(-1, 8, 2 * RADIX), 0)
+            mixed = jnp.dot(am_ref[...], data, preferred_element_type=jnp.float32)
+            line = c * chunk + 2 * pair
+            grid_ref[line] = mixed[:, :RADIX]
+            grid_ref[line + 1] = mixed[:, RADIX:]
+    pltpu.make_async_remote_copy(
+        src_ref=formed.at[:, most],
+        dst_ref=landed.at[:, most],
         send_sem=send_sem,
-        recv_sem=recv_sem,
+        recv_sem=recv_sems.at[0],
         device_id=(group, me),
         device_id_type=MESH_ID,
-    )
-    whole.wait_recv()
-    whole.wait_send()
-    block = pl.ds(pl.multiple_of((me // 8) * 16, 16), 16)
-    shape = (src_ref.shape[0], 16, src_ref.shape[2])
-    mine = lax.broadcasted_iota(jnp.int32, shape, 1) // 2 == me % 8
-    dst_ref[:, block, :] = jnp.where(
-        mine, src_ref[:, block, :].astype(jnp.float32), dst_ref[:, block, :].astype(jnp.float32)
-    ).astype(jnp.bfloat16)
+    ).wait_send()
 
 
 def tables(rate, inverse, tw_ref, tm_ref, q_ref, em_ref, f_ref):
@@ -295,27 +355,14 @@
 
 
 def chain_kernel(
-    rate_ref, x_ref, am_ref, tw_ref, tm_ref, q_ref, em_ref, f_ref, out_ref,
-    grid, mid, held, total, sems,
+    rate_ref, mixed_ref, total_ref, tw_ref, tm_ref, q_ref, em_ref, f_ref, out_ref,
+    grid, mid, held, sems,
 ):
-    total[...] = jnp.zeros_like(total)
-    for pair in range(LINES // 2):
-        tops = [
-            jnp.concatenate([x_ref[h * LINES + 2 * pair], x_ref[h * LINES + 2 * pair + 1]], 1)
-            for h in range(2)
-        ]
-        data = jnp.concatenate(tops, 0)
-        wide = data.astype(jnp.float32)
-        total[...] += jnp.sum((wide * wide).reshape(-1, 8, 2 * RADIX), 0)
-        mixed = jnp.dot(am_ref[...], data, preferred_element_type=jnp.float32)
-        grid[2 * pair] = mixed[:, :RADIX]
-        grid[2 * pair + 1] = mixed[:, RADIX:]
-
     def chan_lines(i, _):
         here = pl.ds(pl.multiple_of(i * 8, 8), 8)
         there = pl.ds(pl.multiple_of(i * 8 + 2 * RADIX, 8), 8)
         values = [
-            times(grid[n, here], grid[n, there], tw_ref[0, n, here], tw_ref[1, n, here])
+            times(mixed_ref[n, here], mixed_ref[n, there], tw_ref[0, n, here], tw_ref[1, n, here])
             for n in range(LINES)
         ]
         for n, (re_part, im_part) in enumerate(sixteen(values, 1)):
@@ -359,7 +406,7 @@
 
     lax.fori_loop(0, RADIX // 8, beat_lines, 0)
 
-    power = jnp.sum(jnp.sum(total[...], 1, keepdims=True), 0, keepdims=True) * (1.0 / LENGTH)
+    power = jnp.sum(jnp.sum(total_ref[...], 1, keepdims=True), 0, keepdims=True) * (1.0 / LENGTH)
     factor = lax.rsqrt(power + EPSILON) * (
         math.sqrt(2.0 / LENGTH) / math.sqrt(CHANS)
     )
@@ -412,41 +459,48 @@
     for _ in range(4):
         inverse = inverse * (2 - rate * inverse)
     rates = jnp.concatenate([rate, inverse & (LENGTH - 1)])
-    block = jax.ShapeDtypeStruct((chan_dev, rows, samples), jnp.bfloat16)
-    formed = pl.pallas_call(
-        form_kernel,
-        out_shape=block,
-        in_specs=[SMEM_SPEC] + [VMEM_SPEC] * 4,
-        out_specs=VMEM_SPEC,
-        scratch_shapes=[pltpu.VMEM((2, rows, 2 * dishes), jnp.float32)] * 2,
-        compiler_params=pltpu.CompilerParams(vmem_limit_bytes=12 << 20),
-        name="form",
-    )(
-        frequency,
-        voltages.reshape(chan_dev, parts * dishes, samples),
-        delays,
-        jnp.repeat(pointing, 2).reshape(1, rows),
-        jnp.tile(dish_mask, 2).reshape(1, 2 * dishes),
-    )
     wide = 2 * RADIX
-    received, tw, tm, q, em, f = pl.pallas_call(
-        functools.partial(exchange_kernel, sizes),
+    chunks = 4
+    mixed, total, tw, tm, q, em, f = pl.pallas_call(
+        functools.partial(front_kernel, sizes),
         out_shape=[
-            block,
+            jax.ShapeDtypeStruct((LINES, 2 * wide, samples), jnp.float32),
+            jax.ShapeDtypeStruct((8, wide), jnp.float32),
             jax.ShapeDtypeStruct((2, LINES, wide, samples), jnp.float32),
             jax.ShapeDtypeStruct((2 * wide, 2 * wide), jnp.bfloat16),
             jax.ShapeDtypeStruct((2, LINES, RADIX, wide), jnp.float32),
             jax.ShapeDtypeStruct((LINES, wide, wide), jnp.bfloat16),
             jax.ShapeDtypeStruct((2, LINES, RADIX, wide), jnp.float32),
         ],
-        in_specs=[SMEM_SPEC, VMEM_SPEC],
-        out_specs=[VMEM_SPEC] * 6,
-        scratch_shapes=[pltpu.SemaphoreType.DMA(())] * 2,
+        in_specs=[SMEM_SPEC] * 2 + [VMEM_SPEC] * 3 + [HBM_SPEC] * 2,
+        out_specs=[VMEM_SPEC] * 7,
+        scratch_shapes=[
+            pltpu.VMEM((chan_dev, parts * dishes, samples), jnp.bfloat16),
+            pltpu.VMEM(delays.shape[::-1], jnp.float32),
+            pltpu.VMEM((2, 2, rows, parts * dishes), jnp.float32),
+            pltpu.VMEM((2, rows, parts * dishes), jnp.float32),
+            pltpu.VMEM((chan_dev, rows, samples), jnp.bfloat16),
+            pltpu.VMEM((chan_dev, rows, samples), jnp.bfloat16),
+            pltpu.SemaphoreType.DMA((chunks, 2)),
+            pltpu.SemaphoreType.DMA(()),
+            pltpu.SemaphoreType.DMA(()),
+            pltpu.SemaphoreType.DMA((chunks,)),
+        ],
         compiler_params=pltpu.CompilerParams(
-            collective_id=0, has_side_effects=True, vmem_limit_bytes=24 << 20
+            collective_id=0, has_side_effects=True, vmem_limit_bytes=20 << 20
         ),
-        name="exchange",
-    )(rates, formed)
+        name="front",
+    )(
+        rates,
+        frequency,
+        pointing.reshape(1, beams),
+        dish_mask.reshape(1, dishes),
+        chan_matrix(members),
+        pltpu.with_memory_space_constraint(
+            voltages.reshape(chan_dev, parts * dishes, samples), pltpu.HBM
+        ),
+        pltpu.with_memory_space_constraint(delays.T, pltpu.HBM),
+    )
     return pl.pallas_call(
         chain_kernel,
         out_shape=jax.ShapeDtypeStruct((1, 2, samples, CHANS), jnp.float32),
@@ -456,12 +510,11 @@
             pltpu.VMEM((LINES, 2 * wide, samples), jnp.float32),
             pltpu.VMEM((LINES, RADIX, 2 * wide), jnp.float32),
             pltpu.VMEM((2, samples, CHANS), jnp.float32),
-            pltpu.VMEM((8, wide), jnp.float32),
             pltpu.SemaphoreType.DMA((LINES,)),
         ],
-        compiler_params=pltpu.CompilerParams(vmem_limit_bytes=36 << 20),
+        compiler_params=pltpu.CompilerParams(vmem_limit_bytes=20 << 20),
         name="chain",
-    )(rates, received, chan_matrix(members), tw, tm, q, em, f)
+    )(rates, mixed, total, tw, tm, q, em, f)
 
 
 def solution(mesh):

time: 102 us -> 90.6 us (0.89)
  the two profiles are of different devices: /device:TPU:721 before, /device:TPU:513 now
where the time goes in v1:
time: 90.6 us; the launch traced here: 90.4 us
  Pallas kernels  87.3 us (96%)
  local copies, waits for them, and re-layouts  2.35 us (3%)
    pallas_call x1, Pallas kernels, on_device(): pl.pallas_call(functools.partial(front_kernel, sizes), out_shape=[jax.Sha...  79.2 us
    pallas_call x1, Pallas kernels, on_device(): pl.pallas_call(chain_kernel, out_shape=jax.ShapeDtypeStruct((1, 2, sample...  8.09 us
    unnamed x6, local copies, waits for them, and re-layouts  2.35 us

profile of v1, /device:TPU:513, one launch (start us, length us, event | category | flops | bytes accessed | tf_op | source)
XLA Modules:
  0.0 90.4 jit_solution(3836941875510704416)
XLA Ops:
  0.7 0.1 pad_add_fusion.rate_ref
  0.7 0.0 copy-start
  0.7 1.0 %copy-done = bf16[512,512]{1,0:T(8,128)(2,1)S(1)} copy-done((bf16[512,512]{1,0:T(8,128)(2,1)S(1)}, bf16[512,512]{1,0:T(8,128)(2,1)}, u32[]{:S(2)}) %copy-start) | copy-done | bytes 524312
  1.8 0.0 copy-start.1
  1.8 0.7 copy-done.1
  2.4 0.0 copy-start.2
  2.4 0.7 copy-done.2
  3.1 79.2 %front.1 = (f32[16,512,128]{2,1,0:T(8,128)S(1)}, f32[8,256]{1,0:T(8,128)S(1)}, f32[2,16,256,128]{3,2,1,0:T(8,128)S(1)}, bf16[512,512]{1,0:T(8,128)(2,1)S(1)}, f3...) custom-call(s32[2]{0:T(128)S(1)} %pad_add_fusion.rate_ref, ...), custom_call_target="tpu_custom_call" | custom-call | tf_op jit(solution)/shard_map/front/pallas_call | solution.py:464
  82.3 8.1 %chain.1 = f32[1,2,128,4096]{3,2,1,0:T(8,128)} custom-call(s32[2]{0:T(128)S(1)} %pad_add_fusion.rate_ref, f32[16,512,128]{2,1,0:T(8,128)S(1)} %get-tuple-element.12.mixed_ref, f32[8,256]{1,0:T(8,128)S(1)} %get-tuple-element.13.total_ref, f32[2,16,256,128]{3,2,1,0:T(8,128)S(1)} %get-tuple-element.14.tw_ref, bf16[512,512]{1,0:T(8,128)(2,1)S(1)} %get-tuple-element.15.tm_ref, ...), custom_call_target="tpu_custom_call" | custom-call | tf_op jit(solution)/shard_map/chain/pallas_call | solution.py:504
Async XLA Ops:
  0.7 1.0 %copy-start = (bf16[512,512]{1,0:T(8,128)(2,1)S(1)}, bf16[512,512]{1,0:T(8,128)(2,1)}, u32[]{:S(2)}) copy-start(bf16[512,512]{1,0:T(8,128)(2,1)} %constant.22.clone.am_ref) | copy-start | bytes 1572868
  1.8 0.7 copy-start.1
  2.4 0.7 copy-start.2

commit v2 on v1

--- a/solution.py
+++ b/solution.py
@@ -24,6 +24,7 @@
 HBM_SPEC = pl.BlockSpec(memory_space=pltpu.HBM)
 LINES = 16
 RADIX = 128
+SPREAD = 45
 
 
 def circle(angle):
@@ -82,31 +83,33 @@
     ]
 
 
+def sixteenth(pair, power, sign):
+    re_part, im_part = pair
+    if power == 0:
+        return pair
+    if power == 4:
+        return (-im_part, re_part) if sign > 0 else (im_part, -re_part)
+    angle = sign * TWO_PI * power / 16
+    return times(re_part, im_part, math.cos(angle), math.sin(angle))
+
+
 def sixteen(values, sign):
     result = [None] * 16
     inner = [four([values[4 * high + low] for high in range(4)], sign) for low in range(4)]
     for first in range(4):
         column = []
         for low in range(4):
-            re_part, im_part = inner[low][first]
-            power = low * first
-            if power == 4:
-                pair = (-im_part, re_part) if sign > 0 else (im_part, -re_part)
-            elif power:
-                angle = sign * TWO_PI * power / 16
-                pair = times(re_part, im_part, math.cos(angle), math.sin(angle))
-            else:
-                pair = (re_part, im_part)
-            column.append(pair)
+            column.append(sixteenth(inner[low][first], low * first, sign))
         for second, pair in enumerate(four(column, sign)):
             result[first + 4 * second] = pair
     return result
 
 
 def front_kernel(
-    sizes, rate_ref, freq_ref, point_ref, mask_ref, am_ref, volt_hbm, table_hbm,
+    sizes, rate_ref, freq_ref, point_hbm, mask_hbm, am_hbm, volt_hbm, table_hbm,
     grid_ref, total_ref, tw_ref, tm_ref, q_ref, em_ref, f_ref,
-    volt, table, wave, step, formed, landed, volt_sems, table_sem, send_sem, recv_sems,
+    volt, table, point_ref, mask_ref, am_ref, wave, step, formed, landed,
+    volt_sems, small_sems, send_sem, recv_sems,
 ):
     rows_y, rows_x, cores = sizes
     members = rows_y * rows_x * cores
@@ -119,17 +122,18 @@
     my_x = (me // cores) % rows_x
     my_core = me % cores
 
-    table_copy = pltpu.make_async_copy(table_hbm, table, table_sem)
-    table_copy.start()
-    volt_copies = []
-    for c in range(chunks):
-        pair = []
-        for half in range(2):
-            here = pl.ds(half * LINES + c * chunk, chunk)
-            copy = pltpu.make_async_copy(volt_hbm.at[here], volt.at[here], volt_sems.at[c, half])
-            copy.start()
-            pair.append(copy)
-        volt_copies.append(pair)
+    small_copies = [
+        pltpu.make_async_copy(point_hbm, point_ref, small_sems.at[0]),
+        pltpu.make_async_copy(table_hbm, table, small_sems.at[1]),
+        pltpu.make_async_copy(mask_hbm, mask_ref, small_sems.at[2]),
+        pltpu.make_async_copy(am_hbm, am_ref, small_sems.at[3]),
+    ]
+    volt_copies = [
+        pltpu.make_async_copy(volt_hbm.at[:, c], volt.at[:, c], volt_sems.at[c])
+        for c in range(chunks)
+    ]
+    for copy in small_copies[:3] + volt_copies + small_copies[3:]:
+        copy.start()
 
     barrier = pltpu.get_barrier_semaphore()
 
@@ -142,7 +146,8 @@
 
     lax.fori_loop(1, members, greet, 0)
 
-    table_copy.wait()
+    for copy in small_copies[:3]:
+        copy.wait()
     rows = formed.shape[1]
     points, beams = table.shape[1], rows // 2
     select = lax.broadcasted_iota(jnp.int32, (points, beams), 0) == point_ref[...]
@@ -165,43 +170,47 @@
     offset = 0.25 * (part_in - part_out).astype(jnp.float32)
     gain = mask_ref[...].astype(jnp.float32) * (1.0 / math.sqrt(dishes))
     gain = jnp.concatenate([gain, gain], 1)
-    for half in range(2):
-        start = freq_ref[0] + half * LINES * BAND_WIDTH / CHANS
-        cosine, sine = circle_turns(start * delay - offset)
-        wave[half, 0] = cosine * gain
-        wave[half, 1] = sine * gain
-    cosine, sine = circle_turns((BAND_WIDTH / CHANS) * delay)
-    step[0] = cosine
-    step[1] = sine
+    def turn(chans):
+        return circle_turns((chans * BAND_WIDTH / CHANS) * delay)
+
+    cosine, sine = circle_turns(freq_ref[0] * delay - offset)
+    wave[0, 0] = cosine * gain
+    wave[0, 1] = sine * gain
+    step[0], step[1] = turn(chunks)
+    for slot in range(1, chunk):
+        wave[slot, 0], wave[slot, 1] = times(
+            wave[slot - 1, 0], wave[slot - 1, 1], step[0], step[1]
+        )
+    step[0], step[1] = turn(LINES)
+    for slot in range(chunk, slots):
+        wave[slot, 0], wave[slot, 1] = times(
+            wave[slot - chunk, 0], wave[slot - chunk, 1], step[0], step[1]
+        )
+    step[0], step[1] = turn(1)
 
     for c in range(chunks):
-        for copy in volt_copies[c]:
-            copy.wait()
-
-        def form(i, _, c=c):
-            for half in range(2):
-                re_part = wave[half, 0]
-                im_part = wave[half, 1]
-                formed[c * slots + half * chunk + i] = jnp.dot(
-                    re_part.astype(jnp.bfloat16),
-                    volt[half * LINES + c * chunk + i],
-                    preferred_element_type=jnp.float32,
-                ).astype(jnp.bfloat16)
-                re_next, im_next = times(re_part, im_part, step[0], step[1])
-                wave[half, 0] = re_next
-                wave[half, 1] = im_next
+        volt_copies[c].wait()
+
+        def form(slot, _, c=c):
+            re_part = wave[slot, 0]
+            im_part = wave[slot, 1]
+            formed[c * slots + slot] = jnp.dot(
+                re_part.astype(jnp.bfloat16), volt[slot, c], preferred_element_type=jnp.float32
+            ).astype(jnp.bfloat16)
+            wave[slot, 0], wave[slot, 1] = times(re_part, im_part, step[0], step[1])
             return 0
 
-        lax.fori_loop(0, chunk, form, 0)
+        lax.fori_loop(0, slots, form, 0)
         if c == 0:
             pl.semaphore_wait(barrier, members - 1)
 
         def send(hop, _, c=c):
-            hop_x = (hop // cores) % rows_x
-            hop_y = (hop // (cores * rows_x) + hop_x) % rows_y
-            to_y = (my_y + hop_y) % rows_y
-            to_x = (my_x + hop_x) % rows_x
-            to = (to_y * rows_x + to_x) * cores + (my_core + hop) % cores
+            place = (hop * SPREAD) % members
+            hop_x = (place // cores) % rows_x
+            hop_y = place // (cores * rows_x)
+            to_y = (my_y + rows_y + hop_y * (1 - 2 * my_core)) % rows_y
+            to_x = (my_x + rows_x + hop_x * (1 - 2 * my_core)) % rows_x
+            to = (to_y * rows_x + to_x) * cores + (my_core + place) % cores
             here = pl.ds(c * slots, slots)
             pltpu.make_async_remote_copy(
                 src_ref=formed.at[here, pl.ds(pl.multiple_of(2 * to, 2), 2)],
@@ -215,6 +224,7 @@
 
         lax.fori_loop(1, members, send, 0)
 
+    small_copies[3].wait()
     tables(rate_ref[0], rate_ref[1], tw_ref, tm_ref, q_ref, em_ref, f_ref)
 
     total_ref[...] = jnp.zeros_like(total_ref)
@@ -249,9 +259,24 @@
             wide = data.astype(jnp.float32)
             total_ref[...] += jnp.sum((wide * wide).reshape(-1, 8, 2 * RADIX), 0)
             mixed = jnp.dot(am_ref[...], data, preferred_element_type=jnp.float32)
-            line = c * chunk + 2 * pair
-            grid_ref[line] = mixed[:, :RADIX]
-            grid_ref[line + 1] = mixed[:, RADIX:]
+            grid_ref[c + 2 * pair * chunks] = mixed[:, :RADIX]
+            grid_ref[c + (2 * pair + 1) * chunks] = mixed[:, RADIX:]
+
+        def chan_fours(i, _, c=c):
+            here = pl.ds(pl.multiple_of(i * 16, 16), 16)
+            there = pl.ds(pl.multiple_of(i * 16 + 2 * RADIX, 16), 16)
+            lines = [c + chunks * high for high in range(4)]
+            values = [
+                times(grid_ref[n, here], grid_ref[n, there], tw_ref[0, n, here], tw_ref[1, n, here])
+                for n in lines
+            ]
+            for first, pair in enumerate(four(values, 1)):
+                re_part, im_part = sixteenth(pair, c * first, 1)
+                grid_ref[lines[first], here] = re_part
+                grid_ref[lines[first], there] = im_part
+            return 0
+
+        lax.fori_loop(0, 2 * RADIX // 16, chan_fours, 0)
     pltpu.make_async_remote_copy(
         src_ref=formed.at[:, most],
         dst_ref=landed.at[:, most],
@@ -361,13 +386,14 @@
     def chan_lines(i, _):
         here = pl.ds(pl.multiple_of(i * 8, 8), 8)
         there = pl.ds(pl.multiple_of(i * 8 + 2 * RADIX, 8), 8)
-        values = [
-            times(mixed_ref[n, here], mixed_ref[n, there], tw_ref[0, n, here], tw_ref[1, n, here])
-            for n in range(LINES)
-        ]
-        for n, (re_part, im_part) in enumerate(sixteen(values, 1)):
-            grid[n, here] = re_part
-            grid[n, there] = im_part
+        for first in range(4):
+            column = [
+                (mixed_ref[low + 4 * first, here], mixed_ref[low + 4 * first, there])
+                for low in range(4)
+            ]
+            for second, (re_part, im_part) in enumerate(four(column, 1)):
+                grid[first + 4 * second, here] = re_part
+                grid[first + 4 * second, there] = im_part
         return 0
 
     lax.fori_loop(0, 2 * RADIX // 8, chan_lines, 0)
@@ -461,6 +487,7 @@
     rates = jnp.concatenate([rate, inverse & (LENGTH - 1)])
     wide = 2 * RADIX
     chunks = 4
+    slots = chan_dev // chunks
     mixed, total, tw, tm, q, em, f = pl.pallas_call(
         functools.partial(front_kernel, sizes),
         out_shape=[
@@ -472,17 +499,20 @@
             jax.ShapeDtypeStruct((LINES, wide, wide), jnp.bfloat16),
             jax.ShapeDtypeStruct((2, LINES, RADIX, wide), jnp.float32),
         ],
-        in_specs=[SMEM_SPEC] * 2 + [VMEM_SPEC] * 3 + [HBM_SPEC] * 2,
+        in_specs=[SMEM_SPEC] * 2 + [HBM_SPEC] * 5,
         out_specs=[VMEM_SPEC] * 7,
         scratch_shapes=[
-            pltpu.VMEM((chan_dev, parts * dishes, samples), jnp.bfloat16),
+            pltpu.VMEM((slots, chunks, parts * dishes, samples), jnp.bfloat16),
             pltpu.VMEM(delays.shape[::-1], jnp.float32),
-            pltpu.VMEM((2, 2, rows, parts * dishes), jnp.float32),
+            pltpu.VMEM((1, beams), jnp.int32),
+            pltpu.VMEM((1, dishes), jnp.int32),
+            pltpu.VMEM((2 * wide, 2 * wide), jnp.bfloat16),
+            pltpu.VMEM((slots, 2, rows, parts * dishes), jnp.float32),
             pltpu.VMEM((2, rows, parts * dishes), jnp.float32),
             pltpu.VMEM((chan_dev, rows, samples), jnp.bfloat16),
             pltpu.VMEM((chan_dev, rows, samples), jnp.bfloat16),
-            pltpu.SemaphoreType.DMA((chunks, 2)),
-            pltpu.SemaphoreType.DMA(()),
+            pltpu.SemaphoreType.DMA((chunks,)),
+            pltpu.SemaphoreType.DMA((4,)),
             pltpu.SemaphoreType.DMA(()),
             pltpu.SemaphoreType.DMA((chunks,)),
         ],
@@ -493,13 +523,16 @@
     )(
         rates,
         frequency,
-        pointing.reshape(1, beams),
-        dish_mask.reshape(1, dishes),
-        chan_matrix(members),
-        pltpu.with_memory_space_constraint(
-            voltages.reshape(chan_dev, parts * dishes, samples), pltpu.HBM
+        *(
+            pltpu.with_memory_space_constraint(value, pltpu.HBM)
+            for value in (
+                pointing.reshape(1, beams),
+                dish_mask.reshape(1, dishes),
+                chan_matrix(members),
+                voltages.reshape(slots, chunks, parts * dishes, samples),
+                delays.T,
+            )
         ),
-        pltpu.with_memory_space_constraint(delays.T, pltpu.HBM),
     )
     return pl.pallas_call(
         chain_kernel,

time: 90.6 us -> 85.4 us (0.943)
  Pallas kernels: 87.3 us -> 84.5 us
  local copies, waits for them, and re-layouts: 2.35 us -> 0 us
    unnamed x6 -> x0, local copies, waits for them, and re-layouts: 2.35 us -> none
    pallas_call x1, Pallas kernels: 79.2 us -> 77.8 us  [on_device(): pl.pallas_call(functools.partial(front_kernel, sizes), out_shape=[jax.Sha...]
    pallas_call x1, Pallas kernels: 8.09 us -> 6.74 us  [on_device(): pl.pallas_call(chain_kernel, out_shape=jax.ShapeDtypeStruct((1, 2, sample...]
where the time goes in v2:
time: 85.4 us; the launch traced here: 85.3 us
  Pallas kernels  84.5 us (99%)
    pallas_call x1, Pallas kernels, on_device(): pl.pallas_call(functools.partial(front_kernel, sizes), out_shape=[jax.Sha...  77.8 us
    pallas_call x1, Pallas kernels, on_device(): pl.pallas_call(chain_kernel, out_shape=jax.ShapeDtypeStruct((1, 2, sample...  6.74 us

profile of v2, /device:TPU:513, one launch (start us, length us, event | category | flops | bytes accessed | tf_op | source)
XLA Modules:
  0.0 85.3 jit_solution(13674988033495746948)
XLA Ops:
  0.7 0.1 pad_add_fusion.rate_ref
  0.7 77.8 %front.1 = (f32[16,512,128]{2,1,0:T(8,128)S(1)}, f32[8,256]{1,0:T(8,128)S(1)}, f32[2,16,256,128]{3,2,1,0:T(8,128)S(1)}, bf16[512,512]{1,0:T(8,128)(2,1)S(1)}, f3...) custom-call(s32[2]{0:T(128)S(1)} %pad_add_fusion.rate_ref, ...), custom_call_target="tpu_custom_call" | custom-call | tf_op jit(solution)/shard_map/front/pallas_call | solution.py:491
  78.5 6.7 %chain.1 = f32[1,2,128,4096]{3,2,1,0:T(8,128)} custom-call(s32[2]{0:T(128)S(1)} %pad_add_fusion.rate_ref, f32[16,512,128]{2,1,0:T(8,128)S(1)} %get-tuple-element.12.mixed_ref, f32[8,256]{1,0:T(8,128)S(1)} %get-tuple-element.13.total_ref, f32[2,16,256,128]{3,2,1,0:T(8,128)S(1)} %get-tuple-element.14.tw_ref, bf16[512,512]{1,0:T(8,128)(2,1)S(1)} %get-tuple-element.15.tm_ref, ...), custom_call_target="tpu_custom_call" | custom-call | tf_op jit(solution)/shard_map/chain/pallas_call | solution.py:537

commit v3 on v2

--- a/solution.py
+++ b/solution.py
@@ -24,6 +24,7 @@
 HBM_SPEC = pl.BlockSpec(memory_space=pltpu.HBM)
 LINES = 16
 RADIX = 128
+GROUPED = 7
 SPREAD = 45
 
 
@@ -112,7 +113,8 @@
     volt_sems, small_sems, send_sem, recv_sems,
 ):
     rows_y, rows_x, cores = sizes
-    members = rows_y * rows_x * cores
+    chips = rows_y * rows_x
+    members = chips * cores
     chunks = recv_sems.shape[0]
     chunk = LINES // chunks
     slots = 2 * chunk
@@ -137,14 +139,20 @@
 
     barrier = pltpu.get_barrier_semaphore()
 
-    def greet(hop, _):
+    def greet(hop):
         pl.semaphore_signal(
             barrier, inc=1, device_id=(group, lax.rem(me + hop, members)),
             device_id_type=MESH_ID,
         )
-        return 0
-
-    lax.fori_loop(1, members, greet, 0)
+
+    def greet_some(i, _):
+        for own in range(GROUPED):
+            greet(1 + i * GROUPED + own)
+        return 0
+
+    lax.fori_loop(0, (members - 1) // GROUPED, greet_some, 0)
+    for hop in range((members - 1) // GROUPED * GROUPED + 1, members):
+        greet(hop)
 
     for copy in small_copies[:3]:
         copy.wait()
@@ -204,13 +212,7 @@
         if c == 0:
             pl.semaphore_wait(barrier, members - 1)
 
-        def send(hop, _, c=c):
-            place = (hop * SPREAD) % members
-            hop_x = (place // cores) % rows_x
-            hop_y = place // (cores * rows_x)
-            to_y = (my_y + rows_y + hop_y * (1 - 2 * my_core)) % rows_y
-            to_x = (my_x + rows_x + hop_x * (1 - 2 * my_core)) % rows_x
-            to = (to_y * rows_x + to_x) * cores + (my_core + place) % cores
+        def send(to, c=c):
             here = pl.ds(c * slots, slots)
             pltpu.make_async_remote_copy(
                 src_ref=formed.at[here, pl.ds(pl.multiple_of(2 * to, 2), 2)],
@@ -220,9 +222,20 @@
                 device_id=(group, to),
                 device_id_type=MESH_ID,
             ).start()
+
+        def send_some(i, _, send=send):
+            for own in range(GROUPED):
+                place = lax.rem((1 + i * GROUPED + own) * SPREAD, chips)
+                to_y = lax.rem(my_y + lax.div(place, rows_x), rows_y)
+                to_x = lax.rem(my_x + lax.rem(place, rows_x), rows_x)
+                chip = (to_y * rows_x + to_x) * cores
+                for core in range(cores):
+                    send(chip + core)
             return 0
 
-        lax.fori_loop(1, members, send, 0)
+        lax.fori_loop(0, (chips - 1) // GROUPED, send_some, 0)
+        for other in range(1, cores):
+            send(me - my_core + lax.rem(my_core + other, cores))
 
     small_copies[3].wait()
     tables(rate_ref[0], rate_ref[1], tw_ref, tm_ref, q_ref, em_ref, f_ref)
@@ -396,7 +409,7 @@
                 grid[first + 4 * second, there] = im_part
         return 0
 
-    lax.fori_loop(0, 2 * RADIX // 8, chan_lines, 0)
+    lax.fori_loop(0, 2 * RADIX // 8, chan_lines, 0, unroll=2)
 
     for quad in range(LINES // 4):
         rows = []
@@ -430,7 +443,7 @@
                 mid[n, here, im_at] = im_part
         return 0
 
-    lax.fori_loop(0, RADIX // 8, beat_lines, 0)
+    lax.fori_loop(0, RADIX // 8, beat_lines, 0, unroll=2)
 
     power = jnp.sum(jnp.sum(total_ref[...], 1, keepdims=True), 0, keepdims=True) * (1.0 / LENGTH)
     factor = lax.rsqrt(power + EPSILON) * (

time: 85.4 us -> 85.1 us (level)
  no operation moved by 1% of the time
where the time goes in v3:
time: 85.1 us; the launch traced here: 85 us
  Pallas kernels  84.2 us (99%)
    pallas_call x1, Pallas kernels, on_device(): pl.pallas_call(functools.partial(front_kernel, sizes), out_shape=[jax.Sha...  77.9 us
    pallas_call x1, Pallas kernels, on_device(): pl.pallas_call(chain_kernel, out_shape=jax.ShapeDtypeStruct((1, 2, sample...  6.33 us

profile of v3, /device:TPU:513, one launch (start us, length us, event | category | flops | bytes accessed | tf_op | source)
XLA Modules:
  0.0 85.0 jit_solution(14246318907537153926)
XLA Ops:
  0.7 0.1 pad_add_fusion.rate_ref
  0.7 77.9 %front.1 = (f32[16,512,128]{2,1,0:T(8,128)S(1)}, f32[8,256]{1,0:T(8,128)S(1)}, f32[2,16,256,128]{3,2,1,0:T(8,128)S(1)}, bf16[512,512]{1,0:T(8,128)(2,1)S(1)}, f3...) custom-call(s32[2]{0:T(128)S(1)} %pad_add_fusion.rate_ref, ...), custom_call_target="tpu_custom_call" | custom-call | tf_op jit(solution)/shard_map/front/pallas_call | solution.py:504
  78.7 6.3 %chain.1 = f32[1,2,128,4096]{3,2,1,0:T(8,128)} custom-call(s32[2]{0:T(128)S(1)} %pad_add_fusion.rate_ref, f32[16,512,128]{2,1,0:T(8,128)S(1)} %get-tuple-element.12.mixed_ref, f32[8,256]{1,0:T(8,128)S(1)} %get-tuple-element.13.total_ref, f32[2,16,256,128]{3,2,1,0:T(8,128)S(1)} %get-tuple-element.14.tw_ref, bf16[512,512]{1,0:T(8,128)(2,1)S(1)} %get-tuple-element.15.tm_ref, ...), custom_call_target="tpu_custom_call" | custom-call | tf_op jit(solution)/shard_map/chain/pallas_call | solution.py:550
